TPU v7x, 8 devices: a whole 2x2x1 slice. The times are simulated.
8 devices in a mesh: replica: 2 (over z, y), data: 4 (over x, core).
Axes of the slice: x: 2, y: 2, z: 1, core: 2. Of those that a mesh axis runs over, the one named last changes fastest.
Arguments:
- x: bfloat16 [4096, 5120], P(('replica', 'data')), parts along dimension 0
- adapter_id: int32 [4096], P(('replica', 'data')), parts along dimension 0
- w_gate: bfloat16 [5120, 13824], replicated
- w_up: bfloat16 [5120, 13824], replicated
- w_down: bfloat16 [13824, 5120], replicated
- a_gate: bfloat16 [64, 5120, 64], P('data')
- b_gate: bfloat16 [64, 64, 13824], P('data')
- a_up: bfloat16 [64, 5120, 64], P('data')
- b_up: bfloat16 [64, 64, 13824], P('data')
- a_down: bfloat16 [64, 13824, 64], P('data')
- b_down: bfloat16 [64, 64, 5120], P('data')
- hot_ids: int32 [4], replicated
- hot_a_gate: bfloat16 [4, 5120, 64], replicated
- hot_b_gate: bfloat16 [4, 64, 13824], replicated
- hot_a_up: bfloat16 [4, 5120, 64], replicated
- hot_b_up: bfloat16 [4, 64, 13824], replicated
- hot_a_down: bfloat16 [4, 13824, 64], replicated
- hot_b_down: bfloat16 [4, 64, 5120], replicated
Outputs:
- output: bfloat16 [4096, 5120], P(('replica', 'data')), parts along dimension 0
There are 2 independent parts. A program takes and returns all parts, laid end to end along the dimension named above; an argument that names none is the same for every part.
All inputs are finite; a program needn't handle non-finite values.
Results may differ from a plain program's by a relative error of at most 0.00183.
Values are sent between devices in bfloat16 or wider.
A program may use at most 2.25 GiB of HBM per device.

v0:
```python
import jax
import jax.numpy as jnp
from jax import lax
from jax.sharding import PartitionSpec as P

value_a10 = 32


def route_layout(tok_ids, hot_ids, group_size, n_local, capacity):
    tok_count = tok_ids.shape[0]
    hot_match = tok_ids[:, None] == hot_ids[None, :]
    is_hot = jnp.any(hot_match, axis=1)
    owner_of = jnp.where(is_hot, group_size, tok_ids // n_local)
    sort_order = jnp.argsort(owner_of, stable=True)
    counts = jax.ops.segment_sum(jnp.ones_like(owner_of), owner_of, num_segments=group_size + 1)
    starts = jnp.cumsum(counts) - counts
    within = jnp.arange(capacity)
    slot_tok = sort_order[jnp.minimum(starts[:group_size, None] + within[None, :], tok_count - 1)].reshape(-1)
    slot_ok = (within[None, :] < counts[:group_size, None]).reshape(-1)
    sort_rank = jnp.zeros_like(owner_of).at[sort_order].set(jnp.arange(tok_count, dtype=owner_of.dtype))
    owner_safe = jnp.minimum(owner_of, group_size - 1)
    tok_slot = owner_safe * capacity + jnp.clip(sort_rank - starts[owner_safe], 0, capacity - 1)
    return hot_match.astype(jnp.bfloat16), is_hot, slot_tok, slot_ok, tok_slot


def adapter_delta(tok_rows, select, a_set, b_set, array_b10):
    low_rank = jnp.einsum("md,ndr->mnr", tok_rows, a_set, preferred_element_type=jnp.float32).astype(jnp.bfloat16)
    low_rank = low_rank * select[:, :, None]
    delta_f = jnp.einsum("mnr,nrf->mf", low_rank, b_set, preferred_element_type=jnp.float32)
    return (array_b10 * delta_f).astype(jnp.bfloat16)


def solution(mesh):
    group_size = mesh.shape["data"]
    token_spec = P(("replica", "data"), None)
    store_spec = P("data", None, None)
    full_mat = P(None, None)
    full_set = P(None, None, None)
    in_specs = (token_spec, P(("replica", "data")), full_mat, full_mat, full_mat) + (store_spec,) * 6 + (P(None),) + (full_set,) * 6

    def device_step(x, adapter_id, w_gate, w_up, w_down, a_gate, b_gate, a_up, b_up, a_down, b_down, hot_ids, hot_a_gate, hot_b_gate, hot_a_up, hot_b_up, hot_a_down, hot_b_down):
        tok_count = x.shape[0]
        n_local = a_gate.shape[0]
        array_b10 = value_a10 / a_gate.shape[2]
        capacity = tok_count // (2 * group_size)
        hot_sel, is_hot, slot_tok, slot_ok, tok_slot = route_layout(adapter_id, hot_ids, group_size, n_local, capacity)

        def exchange(send_rows):
            return lax.all_to_all(send_rows, "data", 0, 0, tiled=True)

        def to_tokens(back_rows):
            return jnp.where(is_hot[:, None], 0.0, jnp.take(back_rows, tok_slot, axis=0).astype(jnp.float32))

        send_ids = jnp.where(slot_ok, jnp.take(adapter_id, slot_tok), -1)
        recv_ids = exchange(send_ids) - lax.axis_index("data") * n_local
        owner_sel = (recv_ids[:, None] == jnp.arange(n_local)[None, :]).astype(jnp.bfloat16)

        recv_x = exchange(jnp.take(x, slot_tok, axis=0))
        gate_back = exchange(adapter_delta(recv_x, owner_sel, a_gate, b_gate, array_b10))
        up_back = exchange(adapter_delta(recv_x, owner_sel, a_up, b_up, array_b10))
        gate_act = (jnp.dot(x, w_gate, preferred_element_type=jnp.float32)
                    + adapter_delta(x, hot_sel, hot_a_gate, hot_b_gate, array_b10).astype(jnp.float32)
                    + to_tokens(gate_back))
        up_act = (jnp.dot(x, w_up, preferred_element_type=jnp.float32)
                  + adapter_delta(x, hot_sel, hot_a_up, hot_b_up, array_b10).astype(jnp.float32)
                  + to_tokens(up_back))
        hidden = (jax.nn.silu(gate_act) * up_act).astype(jnp.bfloat16)

        recv_h = exchange(jnp.take(hidden, slot_tok, axis=0))
        down_back = exchange(adapter_delta(recv_h, owner_sel, a_down, b_down, array_b10))
        down_out = (jnp.dot(hidden, w_down, preferred_element_type=jnp.float32)
                    + adapter_delta(hidden, hot_sel, hot_a_down, hot_b_down, array_b10).astype(jnp.float32)
                    + to_tokens(down_back))
        return (x.astype(jnp.float32) + down_out).astype(jnp.bfloat16)

    return jax.shard_map(device_step, mesh=mesh, in_specs=in_specs, out_specs=token_spec, check_vma=False)
```

profile of v0, /device:TPU:0, one launch (start us, length us, event | category | flops | bytes accessed | tf_op | source)
XLA Modules:
  0.0 734.7 jit_solution(2596339869105342493)
XLA Ops:
  2.7 4.1 scatter_custom_fusion
  7.7 3.8 sort.17
  16.2 4.6 all-to-all-start.1
  20.9 9.3 %gather_fusion.1 = bf16[256,5120]{1,0:T(8,128)(2,1)} fusion(bf16[512,5120]{1,0:T(8,128)(2,1)} %param.20, s32[1024]{0:T(1024)S(1)} %pad_clamp_fusion.1), kind=kCustom, calls=%fused_computation.3 | custom fusion | bytes 5243904 | tf_op jit(solution)/shard_map/jit(_take)/gather | solution.py:58
  33.8 4.8 all-to-all-start
  38.7 30.9 %all-to-all-done = bf16[4,64,5120]{2,1,0:T(8,128)(2,1)} async-done(((bf16[4,64,5120]{2,1,0:T(8,128)(2,1)}), bf16[4,64,5120]{2,1,0:T(8,128)(2,1)}, u32[]{:S(2)}, u32[]{:S(2)}) %all-to-all-start) | async-done | bytes 2621472 | tf_op jit(solution)/shard_map/all_to_all | solution.py:49
  69.7 6.5 fusion.41
  76.1 19.0 %fusion.4 = bf16[256,13824]{1,0:T(8,128)(2,1)} fusion(bf16[16,64,13824]{2,1,0:T(8,128)(2,1)} %param.26, f32[256,16,64]{0,2,1:T(8,128)S(1)} %bitcast.125, bf16[256,16]{0,1:T(8,128)(2,1)S(1)} %fusion.27), kind=kOutput, calls=%fused_computation.18 | convolution fusion | flops 7255359488 | bytes 36446208 | tf_op jit(solution)/shard_map/mnr,nrf->mf/dot_general | solution.py:29
  95.1 5.4 all-to-all-start.2
  100.5 6.5 fusion.43
  107.0 18.9 %fusion.5 = bf16[256,13824]{1,0:T(8,128)(2,1)} fusion(bf16[16,64,13824]{2,1,0:T(8,128)(2,1)} %param.28, f32[256,16,64]{0,2,1:T(8,128)S(1)} %bitcast.124, bf16[256,16]{0,1:T(8,128)(2,1)S(1)} %fusion.27), kind=kOutput, calls=%fused_computation.19 | convolution fusion | flops 7255359488 | bytes 36446208 | tf_op jit(solution)/shard_map/mnr,nrf->mf/dot_general | solution.py:29
  125.9 53.4 %all-to-all-done.2 = bf16[4,64,13824]{2,1,0:T(8,128)(2,1)} async-done(((bf16[4,64,13824]{2,1,0:T(8,128)(2,1)}), bf16[4,64,13824]{2,1,0:T(8,128)(2,1)}, u32[]{:S(2)}, u32[]{:S(2)}) %all-to-all-start.2) | async-done | bytes 7077920 | tf_op jit(solution)/shard_map/all_to_all | solution.py:49
  179.3 5.9 all-to-all-start.3
  185.2 83.2 %fusion.39 = f32[512,13824]{1,0:T(8,128)} fusion(bf16[512,5120]{1,0:T(8,128)(2,1)} %param.20, bf16[5120,13824]{1,0:T(8,128)(2,1)} %param.22), kind=kOutput, calls=%fused_computation.83 | convolution fusion | flops 72477573120 | bytes 175112192 | tf_op jit(solution)/shard_map/dot_general | solution.py:61
  274.7 4.9 fusion.40
  279.6 4.9 fusion.42
  284.4 10.0 %fusion = bf16[512,13824]{1,0:T(8,128)(2,1)} fusion(bf16[4,64,13824]{2,1,0:T(8,128)(2,1)} %param.35, f32[512,4,64]{0,2,1:T(8,128)S(1)} %bitcast.112, bf16[512,4]{0,1:T(4,128)(2,1)S(1)} %copy-done.5), kind=kOutput, calls=%fused_computation.10 | convolution fusion | flops 3638296576 | bytes 21762048 | tf_op jit(solution)/shard_map/mnr,nrf->mf/dot_general | solution.py:29
  294.5 10.0 %fusion.1 = bf16[512,13824]{1,0:T(8,128)(2,1)} fusion(bf16[4,64,13824]{2,1,0:T(8,128)(2,1)} %param.33, f32[512,4,64]{0,2,1:T(8,128)S(1)} %bitcast.111, bf16[512,4]{0,1:T(4,128)(2,1)S(1)} %copy-done.5), kind=kOutput, calls=%fused_computation.12 | convolution fusion | flops 3638296576 | bytes 21762048 | tf_op jit(solution)/shard_map/mnr,nrf->mf/dot_general | solution.py:29
  304.5 29.0 %gather_fusion.5 = bf16[512,13824]{1,0:T(8,128)(2,1)} fusion(bf16[256,13824]{1,0:T(8,128)(2,1)} %bitcast.21, s32[1024]{0:T(1024)S(1)} %pad_clamp_fusion), kind=kCustom, calls=%fused_computation.clone | custom fusion | bytes 28313600 | tf_op jit(solution)/shard_map/jit(_take)/gather | solution.py:52
  333.5 29.1 %gather_fusion.6 = bf16[512,13824]{1,0:T(8,128)(2,1)} fusion(bf16[256,13824]{1,0:T(8,128)(2,1)} %bitcast.31, s32[1024]{0:T(1024)S(1)} %pad_clamp_fusion), kind=kCustom, calls=%fused_computation.1.clone | custom fusion | bytes 28313600 | tf_op jit(solution)/shard_map/jit(_take)/gather | solution.py:52
  362.6 106.1 %multiply_convert_fusion = bf16[512,13824]{1,0:T(8,128)(2,1)} fusion(bf16[512,13824]{1,0:T(8,128)(2,1)} %fusion, f32[512,13824]{1,0:T(8,128)} %fusion.39, bf16[512,13824]{1,0:T(8,128)(2,1)} %fusion.1, bf16[512,5120]{1,0:T(8,128)(2,1)} %param.20, bf16[5120,13824]{1,0:T(8,128)(2,1)} %param.23, bf16[512,13824]{1,0:T(8,128)(2,1)} %gather_fusion.6, ...), kind=kOutput, calls=%fused_computation.13 | convolution fusion | flops 72604975104 | bytes 245892096 | tf_op jit(solution)/shard_map/dot_general | solution.py:64
  468.7 21.4 %gather_fusion.3 = bf16[256,13824]{1,0:T(8,128)(2,1)} fusion(bf16[512,13824]{1,0:T(8,128)(2,1)} %multiply_convert_fusion, s32[1024]{0:T(1024)} %copy-done.13), kind=kCustom, calls=%fused_computation.5 | custom fusion | bytes 14156800 | tf_op jit(solution)/shard_map/jit(_take)/gather | solution.py:69
  490.1 3.7 broadcast_select_fusion
  493.8 82.6 %all_to_all.60 = bf16[4,64,13824]{2,1,0:T(8,128)(2,1)} all-to-all(bf16[4,64,13824]{2,1,0:T(8,128)(2,1)S(1)} %broadcast_select_fusion), channel_id=1, replica_groups=mesh['replica'=2,'data'=4] {'data'}, dimensions={0} | all-to-all | bytes 14155776 | tf_op jit(solution)/shard_map/all_to_all | solution.py:49
  576.4 14.9 %fusion.45 = f32[256,1024]{0,1:S(1)} fusion(bf16[256,13824]{1,0:T(8,128)(2,1)} %bitcast.109, bf16[13824,1024]{0,1:T(8,128)(2,1)} %bitcast.118), kind=kOutput, calls=%fused_computation.89 | convolution fusion | flops 7247757312 | bytes 36438016
  591.4 8.3 %fusion.8 = bf16[256,5120]{1,0:T(8,128)(2,1)} fusion(bf16[16,64,5120]{2,1,0:T(8,128)(2,1)} %param.30, f32[256,16,64]{0,2,1:T(8,128)S(1)} %bitcast.110, bf16[256,16]{0,1:T(8,128)(2,1)S(1)} %copy-done.4), kind=kOutput, calls=%fused_computation.26 | convolution fusion | flops 2687500288 | bytes 14163968 | tf_op jit(solution)/shard_map/mnr,nrf->mf/dot_general | solution.py:29
  599.7 4.6 all-to-all-start.5
  604.3 9.1 %fusion.44 = f32[512,256]{0,1:S(1)} fusion(bf16[512,13824]{1,0:T(8,128)(2,1)} %multiply_convert_fusion, bf16[13824,256]{0,1:T(8,128)(2,1)} %bitcast.121), kind=kOutput, calls=%fused_computation.88 | convolution fusion | flops 3623878656 | bytes 21757952
  613.4 3.9 fusion.6
  617.4 17.9 %all-to-all-done.5 = bf16[4,64,5120]{2,1,0:T(8,128)(2,1)} async-done(((bf16[4,64,5120]{2,1,0:T(8,128)(2,1)}), bf16[4,64,5120]{2,1,0:T(8,128)(2,1)}, u32[]{:S(2)}, u32[]{:S(2)}) %all-to-all-start.5) | async-done | bytes 2621472 | tf_op jit(solution)/shard_map/all_to_all | solution.py:49
  635.3 12.5 %gather_fusion.4 = bf16[512,5120]{1,0:T(8,128)(2,1)} fusion(bf16[256,5120]{1,0:T(8,128)(2,1)} %bitcast.43, s32[1024]{0:T(1024)S(1)} %copy-done.8), kind=kCustom, calls=%fused_computation.6 | custom fusion | bytes 10487808 | tf_op jit(solution)/shard_map/jit(_take)/gather | solution.py:52
  647.8 86.5 %add_convert_fusion = bf16[512,5120]{1,0:T(8,128)(2,1)} fusion(bf16[512,5120]{1,0:T(8,128)(2,1)} %fusion.6, bf16[512,5120]{1,0:T(8,128)(2,1)} %param.20, bf16[512,13824]{1,0:T(8,128)(2,1)} %multiply_convert_fusion, bf16[13824,5120]{1,0:T(8,128)(2,1)} %param.24, bf16[512,5120]{1,0:T(8,128)(2,1)} %gather_fusion.4, pred[512]{0:T(512)(128)(4,1)S(1)} %get-tuple-element.8, ...), kind=kOutput, calls=%fused_computation.22 | convolution fusion | flops 72501166080 | bytes 176686080 | tf_op jit(solution)/shard_map/dot_general | solution.py:71
  (66 shorter events, 18.3 us)
Async XLA Ops:
  0.0 613.4 %copy-start = (bf16[4,64,5120]{2,1,0:T(8,128)(2,1)S(1)}, bf16[4,64,5120]{2,1,0:T(8,128)(2,1)}, u32[]{:S(2)}) copy-start(bf16[4,64,5120]{2,1,0:T(8,128)(2,1)} %param.37) | copy-start | bytes 7864324
  1.5 0.5 copy-start.16
  2.7 8.7 %copy-start.11 = (s32[512]{0:T(512)}, s32[512]{0:T(512)S(1)}, u32[]{:S(2)}) copy-start(s32[512]{0:T(512)S(1)} %fusion.29) | copy-start | bytes 6148
  7.0 0.5 copy-start.9
  11.4 18.8 %copy-start.1 = (s32[512]{0:T(512)}, s32[512]{0:T(512)S(1)}, u32[]{:S(2)}) copy-start(s32[512]{0:T(512)S(1)} %get-tuple-element.7) | copy-start | bytes 6148
  13.5 16.8 %copy-start.13 = (s32[1024]{0:T(1024)}, s32[1024]{0:T(1024)S(1)}, u32[]{:S(2)}) copy-start(s32[1024]{0:T(1024)S(1)} %pad_clamp_fusion.1) | copy-start | bytes 12292
  16.2 17.6 %all-to-all-start.1 = ((s32[4,64,1]{1,2,0:T(1,128)}), s32[4,64,1]{1,2,0:T(1,128)S(1)}, u32[]{:S(2)}, u32[]{:S(2)}) async-start(s32[4,64,1]{1,2,0:T(1,128)} %bitcast.18), calls=%async_computation.1 | async-start | bytes 4096 | tf_op jit(solution)/shard_map/all_to_all | solution.py:49
  20.9 9.4 %copy-start.14 = (pred[4,64]{1,0:T(4,128)(4,1)}, pred[4,64]{1,0:T(4,128)(4,1)S(1)}, u32[]{:S(2)}) copy-start(pred[4,64]{1,0:T(4,128)(4,1)S(1)} %compare_and_fusion.1) | copy-start | bytes 772
  33.8 35.8 %all-to-all-start = ((bf16[4,64,5120]{2,1,0:T(8,128)(2,1)}), bf16[4,64,5120]{2,1,0:T(8,128)(2,1)}, u32[]{:S(2)}, u32[]{:S(2)}) async-start(bf16[4,64,5120]{2,1,0:T(8,128)(2,1)} %broadcast_select_fusion.1), calls=%async_computation | async-start | bytes 5242880 | tf_op jit(solution)/shard_map/all_to_all | solution.py:49
  38.7 68.3 %copy-start.3 = (bf16[256,16]{0,1:T(8,128)(2,1)}, bf16[256,16]{0,1:T(8,128)(2,1)S(1)}, u32[]{:S(2)}) copy-start(bf16[256,16]{0,1:T(8,128)(2,1)S(1)} %fusion.27) | copy-start | bytes 24580
  95.1 84.2 %all-to-all-start.2 = ((bf16[4,64,13824]{2,1,0:T(8,128)(2,1)}), bf16[4,64,13824]{2,1,0:T(8,128)(2,1)}, u32[]{:S(2)}, u32[]{:S(2)}) async-start(bf16[4,64,13824]{2,1,0:T(8,128)(2,1)} %bitcast.108), calls=%async_computation.2 | async-start | bytes 14155776 | tf_op jit(solution)/shard_map/all_to_all | solution.py:49
  179.3 154.2 %all-to-all-start.3 = ((bf16[4,64,13824]{2,1,0:T(8,128)(2,1)}), bf16[4,64,13824]{2,1,0:T(8,128)(2,1)}, u32[]{:S(2)}, u32[]{:S(2)}) async-start(bf16[4,64,13824]{2,1,0:T(8,128)(2,1)} %bitcast.107), calls=%async_computation.3 | async-start | bytes 14155776 | tf_op jit(solution)/shard_map/all_to_all | solution.py:49
  185.2 83.2 %copy-start.2 = (s32[512]{0:T(512)S(1)}, s32[512]{0:T(512)}, u32[]{:S(2)}) copy-start(s32[512]{0:T(512)} %copy-done.1) | copy-start | bytes 6148
  185.2 85.7 %copy-start.10 = (s32[5]{0:T(128)S(1)}, s32[5]{0:T(128)}, u32[]{:S(2)}) copy-start(s32[5]{0:T(128)} %copy-done.9) | copy-start | bytes 64
  185.2 86.4 %copy-start.12 = (s32[512]{0:T(512)S(1)}, s32[512]{0:T(512)}, u32[]{:S(2)}) copy-start(s32[512]{0:T(512)} %copy-done.11) | copy-start | bytes 6148
  268.4 16.0 %copy-start.5 = (bf16[512,4]{0,1:T(4,128)(2,1)S(1)}, bf16[512,4]{0,1:T(4,128)(2,1)}, u32[]{:S(2)}) copy-start(bf16[512,4]{0,1:T(4,128)(2,1)} %get-tuple-element.11) | copy-start | bytes 12292
  274.7 58.8 %copy-start.7 = (s32[1024]{0:T(1024)}, s32[1024]{0:T(1024)S(1)}, u32[]{:S(2)}) copy-start(s32[1024]{0:T(1024)S(1)} %pad_clamp_fusion) | copy-start | bytes 12292
  333.5 29.2 %copy-start.17 = (pred[512]{0:T(512)(128)(4,1)S(1)}, pred[512]{0:T(512)(128)(4,1)}, u32[]{:S(2)}) copy-start(pred[512]{0:T(512)(128)(4,1)} %copy-done.16) | copy-start | bytes 1540
  468.7 21.4 %copy-start.15 = (pred[4,64]{1,0:T(4,128)(4,1)S(1)}, pred[4,64]{1,0:T(4,128)(4,1)}, u32[]{:S(2)}) copy-start(pred[4,64]{1,0:T(4,128)(4,1)} %copy-done.14) | copy-start | bytes 772
  576.4 15.0 %copy-start.4 = (bf16[256,16]{0,1:T(8,128)(2,1)S(1)}, bf16[256,16]{0,1:T(8,128)(2,1)}, u32[]{:S(2)}) copy-start(bf16[256,16]{0,1:T(8,128)(2,1)} %copy-done.3) | copy-start | bytes 24580
  599.7 35.6 %all-to-all-start.5 = ((bf16[4,64,5120]{2,1,0:T(8,128)(2,1)}), bf16[4,64,5120]{2,1,0:T(8,128)(2,1)}, u32[]{:S(2)}, u32[]{:S(2)}) async-start(bf16[4,64,5120]{2,1,0:T(8,128)(2,1)} %bitcast.106), calls=%async_computation.5 | async-start | bytes 5242880 | tf_op jit(solution)/shard_map/all_to_all | solution.py:49
  604.3 9.2 %copy-start.6 = (bf16[512,4]{0,1:T(4,128)(2,1)S(1)}, bf16[512,4]{0,1:T(4,128)(2,1)}, u32[]{:S(2)}) copy-start(bf16[512,4]{0,1:T(4,128)(2,1)} %get-tuple-element.11) | copy-start | bytes 12292
  613.4 21.9 %copy-start.8 = (s32[1024]{0:T(1024)S(1)}, s32[1024]{0:T(1024)}, u32[]{:S(2)}) copy-start(s32[1024]{0:T(1024)} %copy-done.7) | copy-start | bytes 12292
where the time goes:
time: 742 us; the launch traced here: 735 us
  matrix products  393 us (53%)
  local copies, waits for them, and re-layouts  110 us (15%)
  waiting for transfers between devices  102 us (14%)
  blocking collectives  82.6 us (11%)
  starting transfers between devices  25.2 us (3%)
  other arithmetic  21.4 us (3%)
    dot_general x1, matrix products, device_step(): jnp.dot(x, w_up, preferred_element_type=jnp.float32)  106 us
    all_to_all x5, waiting for transfers between devices, exchange(): return lax.all_to_all(send_rows, 'data', 0, 0, tiled=True)  102 us
    dot_general x1, matrix products, device_step(): jnp.dot(hidden, w_down, preferred_element_type=jnp.float32)  86.5 us
    dot_general x1, matrix products, device_step(): jnp.dot(x, w_gate, preferred_element_type=jnp.float32)  83.2 us
    all_to_all x1, blocking collectives, exchange(): return lax.all_to_all(send_rows, 'data', 0, 0, tiled=True)  82.6 us
    gather x3, local copies, waits for them, and re-layouts, to_tokens(): jnp.take(back_rows, tok_slot, axis=0).astype(jnp.float32)  70.7 us
    dot_general x6, matrix products, adapter_delta(): jnp.einsum('mnr,nrf->mf', low_rank, b_set, preferred_element_type=jnp.flo...  70.2 us
    unnamed x6, matrix products  46.8 us
  transfers between devices with their start and end apart: 5, of which 3 were waited for; matrix products, arithmetic and copies ran while one was open for 27% of the time, Pallas kernels for 0%

commit v1 on v0

v1 whole, which is shorter than its diff:
```python
import functools

import jax
import jax.numpy as jnp
from jax import lax
from jax.experimental import pallas as pl
from jax.experimental.pallas import tpu as pltpu
from jax.sharding import PartitionSpec as P

LORA_ALPHA = 32
MESH = pl.DeviceIdType.MESH
BF = jnp.bfloat16
F32 = jnp.float32
NT = (((1,), (1,)), ((), ()))


def dot(a, b):
    return jnp.dot(a, b, preferred_element_type=F32)


def dot_nt(a, b):
    return lax.dot_general(a, b, NT, preferred_element_type=F32)


def peer_of(me, off):
    if off == 1:
        return me + 1 - 2 * (me % 2)
    if off == 2:
        return (me + 2) % 4
    return 3 - me


def route_kernel(n_local, cap, hot_ref, ids_ref, x_ref, xs_ref, sel_ref, back_ref, perm):
    toks = ids_ref.shape[1]
    blocks = 4
    spill = blocks * cap

    @pl.when(pl.program_id(0) == 0)
    def _():
        me = lax.axis_index("data")
        ids = ids_ref[...]
        owner = ids // n_local
        hot_slot = jnp.full_like(ids, -1)
        for j in range(hot_ref.shape[0]):
            hot_slot = jnp.where(ids == hot_ref[j], j, hot_slot)
        is_hot = hot_slot >= 0
        block = jnp.full_like(ids, 3)
        for off in (1, 2, 3):
            block = jnp.where(owner == peer_of(me, off), off - 1, block)
        cat = jnp.where(is_hot, blocks, block)
        onehot = (lax.broadcasted_iota(jnp.int32, (8, toks), 0) == cat).astype(F32)
        upper = (lax.broadcasted_iota(jnp.int32, (toks, toks), 0) < lax.broadcasted_iota(jnp.int32, (toks, toks), 1)).astype(BF)
        before = dot(onehot.astype(BF), upper)
        rank = jnp.sum(onehot * before, axis=0, keepdims=True).astype(jnp.int32)
        counts = jnp.sum(onehot, axis=1, keepdims=True).astype(jnp.int32)
        pos = jnp.where(is_hot, rank, cat * cap + rank)
        start = jnp.zeros((1, 1), jnp.int32)
        hot_pos = jnp.zeros_like(rank)
        for b in range(blocks):
            have = counts[b:b + 1, :]
            fill = cap - have
            hot_pos = jnp.where(rank >= start, b * cap + have + rank - start, hot_pos)
            start = start + fill
        hot_pos = jnp.where(rank >= start, spill + rank - start, hot_pos)
        pos = jnp.where(is_hot, hot_pos, pos)
        place = (lax.broadcasted_iota(jnp.int32, (toks, toks), 0) == pos).astype(F32)
        perm[...] = place.astype(BF)
        back_ref[...] = place.T.astype(BF)
        slot = jnp.where(is_hot, hot_slot, hot_ref.shape[0] + ids % n_local)
        pick = (lax.broadcasted_iota(jnp.int32, (128, toks), 0) == slot).astype(BF)
        sel_ref[...] = dot_nt(place.astype(BF), pick).astype(BF)

    xs_ref[...] = dot(perm[...], x_ref[...]).astype(BF)


def route(x, ids, hot_ids, n_local, cap):
    toks, width = x.shape
    chunk = 1024
    return pl.pallas_call(
        functools.partial(route_kernel, n_local, cap),
        grid=(width // chunk,),
        in_specs=[
            pl.BlockSpec(memory_space=pltpu.SMEM),
            pl.BlockSpec((1, toks), lambda i: (0, 0)),
            pl.BlockSpec((toks, chunk), lambda i: (0, i)),
        ],
        out_specs=[
            pl.BlockSpec((toks, chunk), lambda i: (0, i)),
            pl.BlockSpec((toks, 128), lambda i: (0, 0)),
            pl.BlockSpec((toks, toks), lambda i: (0, 0)),
        ],
        out_shape=[
            jax.ShapeDtypeStruct((toks, width), BF),
            jax.ShapeDtypeStruct((toks, 128), BF),
            jax.ShapeDtypeStruct((toks, toks), BF),
        ],
        scratch_shapes=[pltpu.VMEM((toks, toks), BF)],
    )(hot_ids, ids.reshape(1, toks), x)


def unroute_kernel(back_ref, ys_ref, out_ref):
    out_ref[...] = dot(back_ref[...], ys_ref[...]).astype(BF)


def unroute(back, ys):
    toks, width = ys.shape
    chunk = 1024
    return pl.pallas_call(
        unroute_kernel,
        grid=(width // chunk,),
        in_specs=[pl.BlockSpec((toks, toks), lambda i: (0, 0)), pl.BlockSpec((toks, chunk), lambda i: (0, i))],
        out_specs=pl.BlockSpec((toks, chunk), lambda i: (0, i)),
        out_shape=jax.ShapeDtypeStruct((toks, width), BF),
    )(back, ys)


FB = 256
SLOTS = 3
EARLY = 18


def mlp_kernel(scale, cap,
               xs, sel, wg, wu, wd, agh, agc, bgh, bgc, auh, auc, buh, buc, adh, adc, bdh, bdc,
               ys,
               xv, selv, hv, wbuf, lbuf, abuf, lowg, lowu, lowd, lowacc_h, lowacc_c, acc, ybuf,
               x_sem, xr_send, xr_recv, s_sem, sr_send, sr_recv, w_sem, l_sem, a_sem, y_send, y_recv, y_sem):
    me = lax.axis_index("data")
    toks, d = xs.shape
    f = wg.shape[1]
    half = toks // 2
    kh = agh.shape[0]
    kc = agc.shape[0]
    kk = kh + kc
    fblocks = f // FB
    dblocks = d // FB
    fh = f // 2
    n_gu = EARLY + (fblocks - EARLY) + EARLY
    n_steps = n_gu + 2 * dblocks

    barrier = pltpu.get_barrier_semaphore()
    for off in (1, 2, 3):
        pl.semaphore_signal(barrier, inc=1, device_id={"data": peer_of(me, off)}, device_id_type=MESH)

    def cols(i):
        return pl.ds(pl.multiple_of(i * FB, FB), FB)

    def gu_copies(blk, slot, cold):
        c = cols(blk)
        out = [
            pltpu.make_async_copy(wg.at[:, c], wbuf.at[slot, pl.ds(0, d)], w_sem.at[slot, 0]),
            pltpu.make_async_copy(wu.at[:, c], wbuf.at[slot, pl.ds(d, d)], w_sem.at[slot, 1]),
            pltpu.make_async_copy(bgh.at[:, c], lbuf.at[slot, 0, pl.ds(0, kh)], l_sem.at[slot, 0]),
            pltpu.make_async_copy(buh.at[:, c], lbuf.at[slot, 1, pl.ds(0, kh)], l_sem.at[slot, 1]),
            pltpu.make_async_copy(adh.at[:, c], lbuf.at[slot, 2, pl.ds(0, kh)], l_sem.at[slot, 2]),
        ]
        if cold:
            out += [
                pltpu.make_async_copy(bgc.at[:, c], lbuf.at[slot, 0, pl.ds(kh, kc)], l_sem.at[slot, 3]),
                pltpu.make_async_copy(buc.at[:, c], lbuf.at[slot, 1, pl.ds(kh, kc)], l_sem.at[slot, 4]),
                pltpu.make_async_copy(adc.at[:, c], lbuf.at[slot, 2, pl.ds(kh, kc)], l_sem.at[slot, 5]),
            ]
        return out

    def d_copies(blk, part, slot, low):
        c = cols(blk)
        rows = pl.ds(pl.multiple_of(part * fh, 256), fh)
        out = [pltpu.make_async_copy(wd.at[rows, c], wbuf.at[slot, pl.ds(0, fh)], w_sem.at[slot, 0])]
        if low:
            out += [
                pltpu.make_async_copy(bdh.at[:, c], lbuf.at[slot, 0, pl.ds(0, kh)], l_sem.at[slot, 0]),
                pltpu.make_async_copy(bdc.at[:, c], lbuf.at[slot, 0, pl.ds(kh, kc)], l_sem.at[slot, 3]),
            ]
        return out

    def issue(t):
        slot = t % SLOTS

        @pl.when(t < EARLY)
        def _():
            for c in gu_copies(t, slot, False):
                c.start()

        @pl.when((t >= EARLY) & (t < n_gu))
        def _():
            q = t - EARLY
            j = q // 3
            r = q % 3
            blk = jnp.where(r < 2, EARLY + 2 * j + r, j)
            for c in gu_copies(blk, slot, True):
                c.start()

        @pl.when((t >= n_gu) & (t < n_steps))
        def _():
            q = t - n_gu

            @pl.when(q % 2 == 0)
            def _():
                for c in d_copies(q // 2, 0, slot, False):
                    c.start()

            @pl.when(q % 2 == 1)
            def _():
                for c in d_copies(q // 2, 1, slot, True):
                    c.start()

    def a_copy(i, slot):
        if i < 2:
            src = (agh, auh)[i]
        else:
            c = i - 2
            src = (agc, auc)[c // 4].at[pl.ds((c % 4) * 256, 256)]
        return pltpu.make_async_copy(src, abuf.at[slot], a_sem.at[slot])

    near = pl.ds(half, half)
    far = pl.ds(0, half)
    own = pl.ds(3 * cap, cap)
    local_x = pltpu.make_async_copy(xs.at[near], xv.at[near], x_sem.at[0])
    local_s = pltpu.make_async_copy(sel.at[near], selv.at[near], s_sem.at[0])
    own_x = pltpu.make_async_copy(xs.at[own], xv.at[own], x_sem.at[1])
    own_s = pltpu.make_async_copy(sel.at[own], selv.at[own], s_sem.at[1])
    local_x.start()
    local_s.start()
    a_copy(0, 0).start()
    issue(0)
    a_copy(1, 1).start()
    own_x.start()
    own_s.start()
    a_copy(2, 2).start()
    issue(1)

    pl.semaphore_wait(barrier, 3)
    moves = []
    for off in (2, 3, 1):
        rows = pl.ds((off - 1) * cap, cap)
        for src, dst, snd, rcv in ((sel, selv, sr_send, sr_recv), (xs, xv, xr_send, xr_recv)):
            m = pltpu.make_async_remote_copy(
                src_ref=src.at[rows], dst_ref=dst.at[rows], send_sem=snd.at[off - 1], recv_sem=rcv.at[off - 1],
                device_id={"data": peer_of(me, off)}, device_id_type=MESH)
            m.start()
            moves.append(m)

    def mask(rows, first):
        row = lax.broadcasted_iota(jnp.int32, (128, 256), 0)
        col = lax.broadcasted_iota(jnp.int32, (128, 256), 1)
        spread = (row == first // 64 + col // 64).astype(BF)
        return dot(selv[rows, :], spread).astype(BF)

    def low_x(rows, slot, dst, first):
        low = dot_nt(xv[rows, :], abuf[slot]).astype(BF)
        dst[rows, first:first + 256] = low * mask(rows, first)

    lowacc_h[...] = jnp.zeros_like(lowacc_h)
    lowacc_c[...] = jnp.zeros_like(lowacc_c)
    local_x.wait()
    local_s.wait()
    a_copy(0, 0).wait()
    low_x(near, 0, lowg, 0)
    a_copy(1, 1).wait()
    low_x(near, 1, lowu, 0)

    def delta(low, b):
        return (scale * dot(low, b)).astype(BF).astype(F32)

    def hidden(rows, blk, slot, k):
        g = dot(xv[rows, :], wbuf[slot, 0:d]) + delta(lowg[rows, 0:k], lbuf[slot, 0, 0:k])
        u = dot(xv[rows, :], wbuf[slot, d:2 * d]) + delta(lowu[rows, 0:k], lbuf[slot, 1, 0:k])
        h = (jax.nn.silu(g) * u).astype(BF)
        hv[rows, cols(blk)] = h
        lowacc_h[rows, :] += dot_nt(h, lbuf[slot, 2, 0:kh])
        if k > kh:
            lowacc_c[rows, :] += dot_nt(h, lbuf[slot, 2, kh:kk])

    def early(t, carry):
        slot = t % SLOTS
        issue(t + 2)
        for c in gu_copies(t, slot, False):
            c.wait()
        hidden(near, t, slot, kh)
        return carry

    lax.fori_loop(0, EARLY, early, 0)

    own_x.wait()
    own_s.wait()
    for m in moves:
        m.wait()
    for i in range(10):
        slot = i % 3
        if i >= 2:
            a_copy(i, slot).wait()
        dst = lowg if i == 0 or 2 <= i < 6 else lowu
        first = 0 if i < 2 else 256 * (1 + (i - 2) % 4)
        low_x(far, slot, dst, first)
        if i + 3 < 10:
            a_copy(i + 3, slot).start()

    def group(j, carry):
        def both(r, carry):
            t = EARLY + 3 * j + r
            slot = t % SLOTS
            blk = EARLY + 2 * j + r
            issue(t + 2)
            for c in gu_copies(blk, slot, True):
                c.wait()
            hidden(near, blk, slot, kh)
            hidden(far, blk, slot, kk)
            return carry

        lax.fori_loop(0, 2, both, 0)
        t = EARLY + 3 * j + 2
        slot = t % SLOTS
        issue(t + 2)
        for c in gu_copies(j, slot, True):
            c.wait()
        hidden(far, j, slot, kk)
        return carry

    lax.fori_loop(0, EARLY, group, 0)

    for i in range(kk // 256):
        part = slice(256 * i, 256 * (i + 1))
        if i == 0:
            lowd[near, part] = lowacc_h[near, :].astype(BF) * mask(near, 0)
            lowd[far, part] = lowacc_h[far, :].astype(BF) * mask(far, 0)
        else:
            lowd[far, part] = lowacc_c[:, 256 * (i - 1):256 * i].astype(BF) * mask(far, 256 * i)

    def back_copies(blk):
        p = blk % 2
        c = cols(blk)
        out = []
        for off in (2, 3, 1):
            rows = pl.ds((off - 1) * cap, cap)
            out.append(pltpu.make_async_remote_copy(
                src_ref=ybuf.at[p, rows], dst_ref=ys.at[rows, c], send_sem=y_send.at[p, off - 1],
                recv_sem=y_recv.at[off - 1], device_id={"data": peer_of(me, off)}, device_id_type=MESH))
        mine = pl.ds(3 * cap, toks - 3 * cap)
        return out, pltpu.make_async_copy(ybuf.at[p, mine], ys.at[mine, c], y_sem.at[p])

    def send_back(blk):
        remote, local = back_copies(blk)
        for m in remote:
            m.start()
        local.start()

    def sent(blk):
        remote, local = back_copies(blk)
        for m in remote:
            m.wait_send()
        local.wait()

    def down(i, carry):
        t = n_gu + 2 * i
        slot = t % SLOTS
        issue(t + 2)
        for c in d_copies(i, 0, slot, False):
            c.wait()
        acc[...] = dot(hv[:, 0:fh], wbuf[slot, 0:fh])

        @pl.when(i > 0)
        def _():
            send_back(i - 1)

        t = t + 1
        slot = t % SLOTS
        issue(t + 2)
        for c in d_copies(i, 1, slot, True):
            c.wait()

        @pl.when(i > 1)
        def _():
            sent(i - 2)

        y = acc[...] + dot(hv[:, fh:f], wbuf[slot, 0:fh])
        acc[...] = y
        p = i % 2
        for rows, k in ((near, kh), (far, kk)):
            out = acc[rows, :] + delta(lowd[rows, 0:k], lbuf[slot, 0, 0:k])
            ybuf[p, rows, :] = (xv[rows, cols(i)].astype(F32) + out).astype(BF)
        return carry

    lax.fori_loop(0, dblocks, down, 0)
    send_back(dblocks - 1)
    sent(dblocks - 2)
    sent(dblocks - 1)
    for off in (2, 3, 1):
        rows = pl.ds((off - 1) * cap, cap)
        pltpu.make_async_remote_copy(
            src_ref=ys.at[rows], dst_ref=ys.at[rows], send_sem=y_send.at[0, off - 1], recv_sem=y_recv.at[off - 1],
            device_id={"data": peer_of(me, off)}, device_id_type=MESH).wait_recv()


def mlp(scale, cap, xs, sel, ws, cold, hot):
    toks, d = xs.shape
    f = ws[0].shape[1]
    kh, kc = hot[0].shape[0], cold[0].shape[0]
    kk = kh + kc
    half = toks // 2
    pairs = [m for h, c in zip(hot, cold) for m in (h, c)]
    dma = pltpu.SemaphoreType.DMA
    return pl.pallas_call(
        functools.partial(mlp_kernel, scale, cap),
        in_specs=[pl.BlockSpec(memory_space=pl.ANY)] * 17,
        out_specs=pl.BlockSpec(memory_space=pl.ANY),
        out_shape=jax.ShapeDtypeStruct((toks, d), BF),
        scratch_shapes=[
            pltpu.VMEM((toks, d), BF),
            pltpu.VMEM((toks, 128), BF),
            pltpu.VMEM((toks, f), BF),
            pltpu.VMEM((SLOTS, 2 * d, FB), BF),
            pltpu.VMEM((SLOTS, 3, kk, FB), BF),
            pltpu.VMEM((3, 256, d), BF),
            pltpu.VMEM((toks, kk), BF),
            pltpu.VMEM((toks, kk), BF),
            pltpu.VMEM((toks, kk), BF),
            pltpu.VMEM((toks, kh), F32),
            pltpu.VMEM((half, kc), F32),
            pltpu.VMEM((toks, FB), F32),
            pltpu.VMEM((2, toks, FB), BF),
            dma((2,)), dma((3,)), dma((3,)), dma((2,)), dma((3,)), dma((3,)),
            dma((SLOTS, 2)), dma((SLOTS, 6)), dma((3,)), dma((2, 3)), dma((3,)), dma((2,)),
        ],
        compiler_params=pltpu.CompilerParams(
            collective_id=0, has_side_effects=True, vmem_limit_bytes=63 * 1024 * 1024),
    )(xs, sel, *ws, *pairs)


def solution(mesh):
    group = mesh.shape["data"]
    token_spec = P(("replica", "data"), None)
    store_spec = P("data", None, None)
    full_mat = P(None, None)
    full_set = P(None, None, None)
    in_specs = (token_spec, P(("replica", "data")), full_mat, full_mat, full_mat) + (store_spec,) * 6 + (P(None),) + (full_set,) * 6

    def device_step(x, adapter_id, w_gate, w_up, w_down, a_gate, b_gate, a_up, b_up, a_down, b_down, hot_ids, hot_a_gate, hot_b_gate, hot_a_up, hot_b_up, hot_a_down, hot_b_down):
        cap = x.shape[0] // (2 * group)
        scale = LORA_ALPHA / a_gate.shape[2]

        def flat_a(a):
            return jnp.swapaxes(a, 1, 2).reshape(-1, a.shape[1])

        def flat_b(b):
            return b.reshape(-1, b.shape[2])

        xs, sel, back = route(x, adapter_id, hot_ids, a_gate.shape[0], cap)
        cold = [flat_a(a_gate), flat_b(b_gate), flat_a(a_up), flat_b(b_up), flat_a(a_down), flat_b(b_down)]
        hot = [flat_a(hot_a_gate), flat_b(hot_b_gate), flat_a(hot_a_up), flat_b(hot_b_up), flat_a(hot_a_down), flat_b(hot_b_down)]
        ys = mlp(scale, cap, xs, sel, (w_gate, w_up, w_down), cold, hot)
        return unroute(back, ys)

    return jax.shard_map(device_step, mesh=mesh, in_specs=in_specs, out_specs=token_spec, check_vma=False)
```

time: 742 us -> 430 us (0.58)
  Pallas kernels: 0 us -> 430 us
  matrix products: 393 us -> 0 us
  local copies, waits for them, and re-layouts: 110 us -> 0 us
  waiting for transfers between devices: 102 us -> 0 us
  blocking collectives: 82.6 us -> 0 us
  starting transfers between devices: 25.2 us -> 0 us
  other arithmetic: 21.4 us -> 0 us
    pallas_call x0 -> x3, Pallas kernels: none -> 430 us  [the longest x1 414 us: mlp(): pl.pallas_call(functools.partial(mlp_kernel, scale, cap), in_specs=[pl.Bl...]
    dot_general x9 -> x0, matrix products: 346 us -> none  [the longest x1 106 us: device_step(): jnp.dot(x, w_up, preferred_element_type=jnp.float32)]
    gather x11 -> x0, local copies, waits for them, and re-layouts: 106 us -> none  [the longest x3 70.7 us: to_tokens(): jnp.take(back_rows, tok_slot, axis=0).astype(jnp.float32)]
    all_to_all x5 -> x0, waiting for transfers between devices: 102 us -> none  [exchange(): return lax.all_to_all(send_rows, 'data', 0, 0, tiled=True)]
    all_to_all x1 -> x0, blocking collectives: 82.6 us -> none  [exchange(): return lax.all_to_all(send_rows, 'data', 0, 0, tiled=True)]
    unnamed x6 -> x0, matrix products: 46.8 us -> none
    all_to_all x5 -> x0, starting transfers between devices: 25.2 us -> none  [exchange(): return lax.all_to_all(send_rows, 'data', 0, 0, tiled=True)]
    select_n x7 -> x0, other arithmetic: 8.69 us -> none  [the longest x1 3.75 us: device_step(): recv_h = exchange(jnp.take(hidden, slot_tok, axis=0))]
  transfers between devices with their start and end apart: 5 -> 0, of which waited for: 3 -> 0; matrix products, arithmetic and copies ran while one was open for 27% -> 0% of each run, Pallas kernels for 0% -> 0%
where the time goes in v1:
time: 430 us
  Pallas kernels  430 us (100%)
    pallas_call x1, Pallas kernels, mlp(): pl.pallas_call(functools.partial(mlp_kernel, scale, cap), in_specs=[pl.Bl...  414 us

profile of v1, /device:TPU:0, one launch (start us, length us, event | category | flops | bytes accessed | tf_op | source)
XLA Modules:
  0.0 429.8 jit_solution(14973858918804983345)
XLA Ops:
  0.0 8.2 %shard_map.172 = (bf16[512,5120]{1,0:T(8,128)(2,1)}, bf16[512,128]{1,0:T(8,128)(2,1)}, bf16[512,512]{1,0:T(8,128)(2,1)}) custom-call(s32[4]{0:T(128)} %hot_ref.1, s32[1,512]{1,0:T(1,128)} %bitcast.37, bf16[512,5120]{1,0:T(8,128)(2,1)} %x_ref.1), custom_call_target="tpu_custom_call" | custom-call | tf_op jit(solution)/shard_map/pallas_call | solution.py:79
  8.2 413.9 %shard_map.173.ys_ref = bf16[512,5120]{1,0:T(8,128)(2,1)} custom-call(bf16[512,5120]{1,0:T(8,128)(2,1)} %get-tuple-element.9.xs, bf16[512,128]{1,0:T(8,128)(2,1)} %get-tuple-element.10.sel, bf16[5120,13824]{1,0:T(8,128)(2,1)} %wg.1, bf16[5120,13824]{1,0:T(8,128)(2,1)} %wu.1, bf16[13824,5120]{1,0:T(8,128)(2,1)} %wd.1, bf16[256,5120]{1,0:T(8,128)(2,1)} %bitcast.34, ...), custom_call_target="tpu_custom_call" | custom-call | tf_op jit(solution)/shard_map/pallas_call | solution.py:401
  422.1 7.7 %shard_map.174 = bf16[512,5120]{1,0:T(8,128)(2,1)} custom-call(bf16[512,512]{1,0:T(8,128)(2,1)} %get-tuple-element.8.back_ref, bf16[512,5120]{1,0:T(8,128)(2,1)} %shard_map.173.ys_ref), custom_call_target="tpu_custom_call" | custom-call | tf_op jit(solution)/shard_map/pallas_call | solution.py:108

commit v2 on v1

--- a/solution.py
+++ b/solution.py
@@ -117,13 +117,14 @@
 FB = 256
 SLOTS = 3
 EARLY = 18
+AD_STEPS = 6
 
 
 def mlp_kernel(scale, cap,
                xs, sel, wg, wu, wd, agh, agc, bgh, bgc, auh, auc, buh, buc, adh, adc, bdh, bdc,
                ys,
-               xv, selv, hv, wbuf, lbuf, abuf, lowg, lowu, lowd, lowacc_h, lowacc_c, acc, ybuf,
-               x_sem, xr_send, xr_recv, s_sem, sr_send, sr_recv, w_sem, l_sem, a_sem, y_send, y_recv, y_sem):
+               xv, selv, hv, wbuf, lbuf, abuf, lowg, lowu, lowacc_h, lowacc_c, ybuf,
+               x_sem, xr_send, xr_recv, s_sem, sr_send, sr_recv, w_sem, l_sem, d_sem, a_sem, y_send, y_recv, y_sem):
     me = lax.axis_index("data")
     toks, d = xs.shape
     f = wg.shape[1]
@@ -133,9 +134,10 @@
     kk = kh + kc
     fblocks = f // FB
     dblocks = d // FB
-    fh = f // 2
+    per = fblocks // AD_STEPS
     n_gu = EARLY + (fblocks - EARLY) + EARLY
-    n_steps = n_gu + 2 * dblocks
+    n_ad = n_gu + AD_STEPS
+    n_steps = n_ad + dblocks
 
     barrier = pltpu.get_barrier_semaphore()
     for off in (1, 2, 3):
@@ -151,26 +153,29 @@
             pltpu.make_async_copy(wu.at[:, c], wbuf.at[slot, pl.ds(d, d)], w_sem.at[slot, 1]),
             pltpu.make_async_copy(bgh.at[:, c], lbuf.at[slot, 0, pl.ds(0, kh)], l_sem.at[slot, 0]),
             pltpu.make_async_copy(buh.at[:, c], lbuf.at[slot, 1, pl.ds(0, kh)], l_sem.at[slot, 1]),
-            pltpu.make_async_copy(adh.at[:, c], lbuf.at[slot, 2, pl.ds(0, kh)], l_sem.at[slot, 2]),
         ]
         if cold:
             out += [
-                pltpu.make_async_copy(bgc.at[:, c], lbuf.at[slot, 0, pl.ds(kh, kc)], l_sem.at[slot, 3]),
-                pltpu.make_async_copy(buc.at[:, c], lbuf.at[slot, 1, pl.ds(kh, kc)], l_sem.at[slot, 4]),
-                pltpu.make_async_copy(adc.at[:, c], lbuf.at[slot, 2, pl.ds(kh, kc)], l_sem.at[slot, 5]),
+                pltpu.make_async_copy(bgc.at[:, c], lbuf.at[slot, 0, pl.ds(kh, kc)], l_sem.at[slot, 2]),
+                pltpu.make_async_copy(buc.at[:, c], lbuf.at[slot, 1, pl.ds(kh, kc)], l_sem.at[slot, 3]),
             ]
         return out
 
-    def d_copies(blk, part, slot, low):
+    def ad_copies(blk, slot):
+        out = []
+        for q in range(per):
+            c = cols(blk * per + q)
+            out.append(pltpu.make_async_copy(adh.at[:, c], wbuf.at[slot, pl.ds(q * kk, kh)], d_sem.at[slot, 2 * q]))
+            out.append(pltpu.make_async_copy(adc.at[:, c], wbuf.at[slot, pl.ds(q * kk + kh, kc)], d_sem.at[slot, 2 * q + 1]))
+        return out
+
+    def d_copies(blk, slot):
         c = cols(blk)
-        rows = pl.ds(pl.multiple_of(part * fh, 256), fh)
-        out = [pltpu.make_async_copy(wd.at[rows, c], wbuf.at[slot, pl.ds(0, fh)], w_sem.at[slot, 0])]
-        if low:
-            out += [
-                pltpu.make_async_copy(bdh.at[:, c], lbuf.at[slot, 0, pl.ds(0, kh)], l_sem.at[slot, 0]),
-                pltpu.make_async_copy(bdc.at[:, c], lbuf.at[slot, 0, pl.ds(kh, kc)], l_sem.at[slot, 3]),
-            ]
-        return out
+        return [
+            pltpu.make_async_copy(wd.at[:, c], wbuf.at[slot], w_sem.at[slot, 0]),
+            pltpu.make_async_copy(bdh.at[:, c], lbuf.at[slot, 0, pl.ds(0, kh)], l_sem.at[slot, 0]),
+            pltpu.make_async_copy(bdc.at[:, c], lbuf.at[slot, 0, pl.ds(kh, kc)], l_sem.at[slot, 2]),
+        ]
 
     def issue(t):
         slot = t % SLOTS
@@ -189,19 +194,15 @@
             for c in gu_copies(blk, slot, True):
                 c.start()
 
-        @pl.when((t >= n_gu) & (t < n_steps))
-        def _():
-            q = t - n_gu
-
-            @pl.when(q % 2 == 0)
-            def _():
-                for c in d_copies(q // 2, 0, slot, False):
-                    c.start()
-
-            @pl.when(q % 2 == 1)
-            def _():
-                for c in d_copies(q // 2, 1, slot, True):
-                    c.start()
+        @pl.when((t >= n_gu) & (t < n_ad))
+        def _():
+            for c in ad_copies(t - n_gu, slot):
+                c.start()
+
+        @pl.when((t >= n_ad) & (t < n_steps))
+        def _():
+            for c in d_copies(t - n_ad, slot):
+                c.start()
 
     def a_copy(i, slot):
         if i < 2:
@@ -264,11 +265,7 @@
     def hidden(rows, blk, slot, k):
         g = dot(xv[rows, :], wbuf[slot, 0:d]) + delta(lowg[rows, 0:k], lbuf[slot, 0, 0:k])
         u = dot(xv[rows, :], wbuf[slot, d:2 * d]) + delta(lowu[rows, 0:k], lbuf[slot, 1, 0:k])
-        h = (jax.nn.silu(g) * u).astype(BF)
-        hv[rows, cols(blk)] = h
-        lowacc_h[rows, :] += dot_nt(h, lbuf[slot, 2, 0:kh])
-        if k > kh:
-            lowacc_c[rows, :] += dot_nt(h, lbuf[slot, 2, kh:kk])
+        hv[rows, cols(blk)] = (jax.nn.silu(g) * u).astype(BF)
 
     def early(t, carry):
         slot = t % SLOTS
@@ -317,6 +314,25 @@
 
     lax.fori_loop(0, EARLY, group, 0)
 
+    def low_h(i, carry):
+        t = n_gu + i
+        slot = t % SLOTS
+        issue(t + 2)
+        for c in ad_copies(i, slot):
+            c.wait()
+        first = i * per
+        hot_sum, cold_sum = lowacc_h[...], lowacc_c[...]
+        for q in range(per):
+            c = cols(first + q)
+            hot_sum += dot_nt(hv[:, c], wbuf[slot, q * kk:q * kk + kh])
+            cold_sum += dot_nt(hv[far, c], wbuf[slot, q * kk + kh:(q + 1) * kk])
+        lowacc_h[...] = hot_sum
+        lowacc_c[...] = cold_sum
+        return carry
+
+    lax.fori_loop(0, AD_STEPS, low_h, 0)
+
+    lowd = lowg
     for i in range(kk // 256):
         part = slice(256 * i, 256 * (i + 1))
         if i == 0:
@@ -350,33 +366,24 @@
         local.wait()
 
     def down(i, carry):
-        t = n_gu + 2 * i
+        t = n_ad + i
         slot = t % SLOTS
+
+        @pl.when(i > 0)
+        def _():
+            send_back(i - 1)
+
+        @pl.when(i > 1)
+        def _():
+            sent(i - 2)
+
         issue(t + 2)
-        for c in d_copies(i, 0, slot, False):
+        for c in d_copies(i, slot):
             c.wait()
-        acc[...] = dot(hv[:, 0:fh], wbuf[slot, 0:fh])
-
-        @pl.when(i > 0)
-        def _():
-            send_back(i - 1)
-
-        t = t + 1
-        slot = t % SLOTS
-        issue(t + 2)
-        for c in d_copies(i, 1, slot, True):
-            c.wait()
-
-        @pl.when(i > 1)
-        def _():
-            sent(i - 2)
-
-        y = acc[...] + dot(hv[:, fh:f], wbuf[slot, 0:fh])
-        acc[...] = y
         p = i % 2
         for rows, k in ((near, kh), (far, kk)):
-            out = acc[rows, :] + delta(lowd[rows, 0:k], lbuf[slot, 0, 0:k])
-            ybuf[p, rows, :] = (xv[rows, cols(i)].astype(F32) + out).astype(BF)
+            y = dot(hv[rows, :], wbuf[slot]) + delta(lowd[rows, 0:k], lbuf[slot, 0, 0:k])
+            ybuf[p, rows, :] = (xv[rows, cols(i)].astype(F32) + y).astype(BF)
         return carry
 
     lax.fori_loop(0, dblocks, down, 0)
@@ -407,18 +414,16 @@
             pltpu.VMEM((toks, d), BF),
             pltpu.VMEM((toks, 128), BF),
             pltpu.VMEM((toks, f), BF),
-            pltpu.VMEM((SLOTS, 2 * d, FB), BF),
-            pltpu.VMEM((SLOTS, 3, kk, FB), BF),
+            pltpu.VMEM((SLOTS, f, FB), BF),
+            pltpu.VMEM((SLOTS, 2, kk, FB), BF),
             pltpu.VMEM((3, 256, d), BF),
-            pltpu.VMEM((toks, kk), BF),
             pltpu.VMEM((toks, kk), BF),
             pltpu.VMEM((toks, kk), BF),
             pltpu.VMEM((toks, kh), F32),
             pltpu.VMEM((half, kc), F32),
-            pltpu.VMEM((toks, FB), F32),
             pltpu.VMEM((2, toks, FB), BF),
             dma((2,)), dma((3,)), dma((3,)), dma((2,)), dma((3,)), dma((3,)),
-            dma((SLOTS, 2)), dma((SLOTS, 6)), dma((3,)), dma((2, 3)), dma((3,)), dma((2,)),
+            dma((SLOTS, 2)), dma((SLOTS, 4)), dma((SLOTS, 2 * (f // FB // AD_STEPS))), dma((3,)), dma((2, 3)), dma((3,)), dma((2,)),
         ],
         compiler_params=pltpu.CompilerParams(
             collective_id=0, has_side_effects=True, vmem_limit_bytes=63 * 1024 * 1024),

time: 430 us -> 324 us (0.75)
  Pallas kernels: 430 us -> 324 us
    pallas_call x1, Pallas kernels: 414 us -> 308 us  [mlp(): pl.pallas_call(functools.partial(mlp_kernel, scale, cap), in_specs=[pl.Bl...]
where the time goes in v2:
time: 324 us
  Pallas kernels  324 us (100%)
    pallas_call x1, Pallas kernels, mlp(): pl.pallas_call(functools.partial(mlp_kernel, scale, cap), in_specs=[pl.Bl...  308 us
    pallas_call x1, Pallas kernels, route(): pl.pallas_call(functools.partial(route_kernel, n_local, cap), grid=(width...  8.18 us
    pallas_call x1, Pallas kernels, unroute(): pl.pallas_call(unroute_kernel, grid=(width // chunk,), in_specs=[pl.Block...  7.73 us

profile of v2, /device:TPU:0, one launch (start us, length us, event | category | flops | bytes accessed | tf_op | source)
XLA Modules:
  0.0 323.7 jit_solution(17360661720345179067)
XLA Ops:
  0.0 8.2 %shard_map.172 = (bf16[512,5120]{1,0:T(8,128)(2,1)}, bf16[512,128]{1,0:T(8,128)(2,1)}, bf16[512,512]{1,0:T(8,128)(2,1)}) custom-call(s32[4]{0:T(128)} %hot_ref.1, s32[1,512]{1,0:T(1,128)} %bitcast.37, bf16[512,5120]{1,0:T(8,128)(2,1)} %x_ref.1), custom_call_target="tpu_custom_call" | custom-call | tf_op jit(solution)/shard_map/pallas_call | solution.py:79
  8.2 307.8 %shard_map.173.ys_ref = bf16[512,5120]{1,0:T(8,128)(2,1)} custom-call(bf16[512,5120]{1,0:T(8,128)(2,1)} %get-tuple-element.9.xs, bf16[512,128]{1,0:T(8,128)(2,1)} %get-tuple-element.10.sel, bf16[5120,13824]{1,0:T(8,128)(2,1)} %wg.1, bf16[5120,13824]{1,0:T(8,128)(2,1)} %wu.1, bf16[13824,5120]{1,0:T(8,128)(2,1)} %wd.1, bf16[256,5120]{1,0:T(8,128)(2,1)} %bitcast.34, ...), custom_call_target="tpu_custom_call" | custom-call | tf_op jit(solution)/shard_map/pallas_call | solution.py:408
  316.0 7.7 %shard_map.174 = bf16[512,5120]{1,0:T(8,128)(2,1)} custom-call(bf16[512,512]{1,0:T(8,128)(2,1)} %get-tuple-element.8.back_ref, bf16[512,5120]{1,0:T(8,128)(2,1)} %shard_map.173.ys_ref), custom_call_target="tpu_custom_call" | custom-call | tf_op jit(solution)/shard_map/pallas_call | solution.py:108

commit v3 on v2

--- a/solution.py
+++ b/solution.py
@@ -30,72 +30,35 @@
     return 3 - me
 
 
-def route_kernel(n_local, cap, hot_ref, ids_ref, x_ref, xs_ref, sel_ref, back_ref, perm):
-    toks = ids_ref.shape[1]
+def placement(me, n_local, cap, hot_ref, ids):
+    toks = ids.shape[1]
     blocks = 4
-    spill = blocks * cap
-
-    @pl.when(pl.program_id(0) == 0)
-    def _():
-        me = lax.axis_index("data")
-        ids = ids_ref[...]
-        owner = ids // n_local
-        hot_slot = jnp.full_like(ids, -1)
-        for j in range(hot_ref.shape[0]):
-            hot_slot = jnp.where(ids == hot_ref[j], j, hot_slot)
-        is_hot = hot_slot >= 0
-        block = jnp.full_like(ids, 3)
-        for off in (1, 2, 3):
-            block = jnp.where(owner == peer_of(me, off), off - 1, block)
-        cat = jnp.where(is_hot, blocks, block)
-        onehot = (lax.broadcasted_iota(jnp.int32, (8, toks), 0) == cat).astype(F32)
-        upper = (lax.broadcasted_iota(jnp.int32, (toks, toks), 0) < lax.broadcasted_iota(jnp.int32, (toks, toks), 1)).astype(BF)
-        before = dot(onehot.astype(BF), upper)
-        rank = jnp.sum(onehot * before, axis=0, keepdims=True).astype(jnp.int32)
-        counts = jnp.sum(onehot, axis=1, keepdims=True).astype(jnp.int32)
-        pos = jnp.where(is_hot, rank, cat * cap + rank)
-        start = jnp.zeros((1, 1), jnp.int32)
-        hot_pos = jnp.zeros_like(rank)
-        for b in range(blocks):
-            have = counts[b:b + 1, :]
-            fill = cap - have
-            hot_pos = jnp.where(rank >= start, b * cap + have + rank - start, hot_pos)
-            start = start + fill
-        hot_pos = jnp.where(rank >= start, spill + rank - start, hot_pos)
-        pos = jnp.where(is_hot, hot_pos, pos)
-        place = (lax.broadcasted_iota(jnp.int32, (toks, toks), 0) == pos).astype(F32)
-        perm[...] = place.astype(BF)
-        back_ref[...] = place.T.astype(BF)
-        slot = jnp.where(is_hot, hot_slot, hot_ref.shape[0] + ids % n_local)
-        pick = (lax.broadcasted_iota(jnp.int32, (128, toks), 0) == slot).astype(BF)
-        sel_ref[...] = dot_nt(place.astype(BF), pick).astype(BF)
-
-    xs_ref[...] = dot(perm[...], x_ref[...]).astype(BF)
-
-
-def route(x, ids, hot_ids, n_local, cap):
-    toks, width = x.shape
-    chunk = 1024
-    return pl.pallas_call(
-        functools.partial(route_kernel, n_local, cap),
-        grid=(width // chunk,),
-        in_specs=[
-            pl.BlockSpec(memory_space=pltpu.SMEM),
-            pl.BlockSpec((1, toks), lambda i: (0, 0)),
-            pl.BlockSpec((toks, chunk), lambda i: (0, i)),
-        ],
-        out_specs=[
-            pl.BlockSpec((toks, chunk), lambda i: (0, i)),
-            pl.BlockSpec((toks, 128), lambda i: (0, 0)),
-            pl.BlockSpec((toks, toks), lambda i: (0, 0)),
-        ],
-        out_shape=[
-            jax.ShapeDtypeStruct((toks, width), BF),
-            jax.ShapeDtypeStruct((toks, 128), BF),
-            jax.ShapeDtypeStruct((toks, toks), BF),
-        ],
-        scratch_shapes=[pltpu.VMEM((toks, toks), BF)],
-    )(hot_ids, ids.reshape(1, toks), x)
+    owner = ids // n_local
+    hot_slot = jnp.full_like(ids, -1)
+    for j in range(hot_ref.shape[0]):
+        hot_slot = jnp.where(ids == hot_ref[j], j, hot_slot)
+    is_hot = hot_slot >= 0
+    block = jnp.full_like(ids, 3)
+    for off in (1, 2, 3):
+        block = jnp.where(owner == peer_of(me, off), off - 1, block)
+    cat = jnp.where(is_hot, blocks, block)
+    onehot = (lax.broadcasted_iota(jnp.int32, (8, toks), 0) == cat).astype(F32)
+    upper = (lax.broadcasted_iota(jnp.int32, (toks, toks), 0) < lax.broadcasted_iota(jnp.int32, (toks, toks), 1)).astype(BF)
+    before = dot(onehot.astype(BF), upper)
+    rank = jnp.sum(onehot * before, axis=0, keepdims=True).astype(jnp.int32)
+    counts = jnp.sum(onehot, axis=1, keepdims=True).astype(jnp.int32)
+    start = jnp.zeros((1, 1), jnp.int32)
+    hot_pos = jnp.zeros_like(rank)
+    for b in range(blocks):
+        have = counts[b:b + 1, :]
+        hot_pos = jnp.where(rank >= start, b * cap + have + rank - start, hot_pos)
+        start = start + cap - have
+    hot_pos = jnp.where(rank >= start, blocks * cap + rank - start, hot_pos)
+    pos = jnp.where(is_hot, hot_pos, cat * cap + rank)
+    place = (lax.broadcasted_iota(jnp.int32, (toks, toks), 0) == pos).astype(F32)
+    slot = jnp.where(is_hot, hot_slot, hot_ref.shape[0] + ids % n_local)
+    pick = (lax.broadcasted_iota(jnp.int32, (128, toks), 0) == slot).astype(BF)
+    return place, pick
 
 
 def unroute_kernel(back_ref, ys_ref, out_ref):
@@ -104,7 +67,7 @@
 
 def unroute(back, ys):
     toks, width = ys.shape
-    chunk = 1024
+    chunk = 1280
     return pl.pallas_call(
         unroute_kernel,
         grid=(width // chunk,),
@@ -120,13 +83,13 @@
 AD_STEPS = 6
 
 
-def mlp_kernel(scale, cap,
-               xs, sel, wg, wu, wd, agh, agc, bgh, bgc, auh, auc, buh, buc, adh, adc, bdh, bdc,
-               ys,
-               xv, selv, hv, wbuf, lbuf, abuf, lowg, lowu, lowacc_h, lowacc_c, ybuf,
-               x_sem, xr_send, xr_recv, s_sem, sr_send, sr_recv, w_sem, l_sem, d_sem, a_sem, y_send, y_recv, y_sem):
+def mlp_kernel(scale, cap, n_local,
+               hot_ids, ids, x, wg, wu, wd, agh, agc, bgh, bgc, auh, auc, buh, buc, adh, adc, bdh, bdc,
+               ys, back,
+               xv, selv, sels, perm, backv, hv, wbuf, lbuf, abuf, lowg, lowu, lowacc_h, lowacc_c, ybuf,
+               x_sem, b_sem, xr_send, xr_recv, sr_send, sr_recv, w_sem, l_sem, d_sem, a_sem, y_send, y_recv, y_sem):
     me = lax.axis_index("data")
-    toks, d = xs.shape
+    toks, d = x.shape
     f = wg.shape[1]
     half = toks // 2
     kh = agh.shape[0]
@@ -215,17 +178,25 @@
     near = pl.ds(half, half)
     far = pl.ds(0, half)
     own = pl.ds(3 * cap, cap)
-    local_x = pltpu.make_async_copy(xs.at[near], xv.at[near], x_sem.at[0])
-    local_s = pltpu.make_async_copy(sel.at[near], selv.at[near], s_sem.at[0])
-    own_x = pltpu.make_async_copy(xs.at[own], xv.at[own], x_sem.at[1])
-    own_s = pltpu.make_async_copy(sel.at[own], selv.at[own], s_sem.at[1])
-    local_x.start()
-    local_s.start()
+    chunk = 1024
+    loads = [pltpu.make_async_copy(x.at[:, pl.ds(c, chunk)], hv.at[:, pl.ds(d + c, chunk)], x_sem.at[c // chunk])
+             for c in range(0, d, chunk)]
+    for c in loads:
+        c.start()
     a_copy(0, 0).start()
+    a_copy(1, 1).start()
     issue(0)
-    a_copy(1, 1).start()
-    own_x.start()
-    own_s.start()
+    place, pick = placement(me, n_local, cap, hot_ids, ids[...])
+    perm[...] = place.astype(BF)
+    for c, load in zip(range(0, d, chunk), loads):
+        load.wait()
+        rows = dot(perm[0:half, :], hv[:, d + c:d + c + chunk]).astype(BF)
+        hv[far, c:c + chunk] = rows
+        xv[own, c:c + chunk] = rows[3 * cap:, :]
+    sel = dot_nt(perm[...], pick).astype(BF)
+    sels[...] = sel[0:half, :]
+    selv[3 * cap:toks, :] = sel[3 * cap:, :]
+    backv[...] = place.T.astype(BF)
     a_copy(2, 2).start()
     issue(1)
 
@@ -233,12 +204,16 @@
     moves = []
     for off in (2, 3, 1):
         rows = pl.ds((off - 1) * cap, cap)
-        for src, dst, snd, rcv in ((sel, selv, sr_send, sr_recv), (xs, xv, xr_send, xr_recv)):
+        for src, dst, snd, rcv in ((sels.at[rows], selv, sr_send, sr_recv), (hv.at[rows, pl.ds(0, d)], xv, xr_send, xr_recv)):
             m = pltpu.make_async_remote_copy(
-                src_ref=src.at[rows], dst_ref=dst.at[rows], send_sem=snd.at[off - 1], recv_sem=rcv.at[off - 1],
+                src_ref=src, dst_ref=dst.at[rows], send_sem=snd.at[off - 1], recv_sem=rcv.at[off - 1],
                 device_id={"data": peer_of(me, off)}, device_id_type=MESH)
             m.start()
             moves.append(m)
+    keep_back = pltpu.make_async_copy(backv, back, b_sem)
+    keep_back.start()
+    for c in range(0, d, chunk):
+        xv[near, c:c + chunk] = dot(perm[half:toks, :], hv[:, d + c:d + c + chunk]).astype(BF)
 
     def mask(rows, first):
         row = lax.broadcasted_iota(jnp.int32, (128, 256), 0)
@@ -252,8 +227,6 @@
 
     lowacc_h[...] = jnp.zeros_like(lowacc_h)
     lowacc_c[...] = jnp.zeros_like(lowacc_c)
-    local_x.wait()
-    local_s.wait()
     a_copy(0, 0).wait()
     low_x(near, 0, lowg, 0)
     a_copy(1, 1).wait()
@@ -277,8 +250,7 @@
 
     lax.fori_loop(0, EARLY, early, 0)
 
-    own_x.wait()
-    own_s.wait()
+    keep_back.wait()
     for m in moves:
         m.wait()
     for i in range(10):
@@ -365,6 +337,11 @@
             m.wait_send()
         local.wait()
 
+    def down_rows(i, slot, first, count, k):
+        rows = pl.ds(first, count)
+        y = dot(hv[rows, :], wbuf[slot]) + delta(lowd[rows, 0:k], lbuf[slot, 0, 0:k])
+        ybuf[i % 2, rows, :] = (xv[rows, cols(i)].astype(F32) + y).astype(BF)
+
     def down(i, carry):
         t = n_ad + i
         slot = t % SLOTS
@@ -380,16 +357,26 @@
         issue(t + 2)
         for c in d_copies(i, slot):
             c.wait()
-        p = i % 2
-        for rows, k in ((near, kh), (far, kk)):
-            y = dot(hv[rows, :], wbuf[slot]) + delta(lowd[rows, 0:k], lbuf[slot, 0, 0:k])
-            ybuf[p, rows, :] = (xv[rows, cols(i)].astype(F32) + y).astype(BF)
+        down_rows(i, slot, half, half, kh)
+        down_rows(i, slot, 0, half, kk)
         return carry
 
-    lax.fori_loop(0, dblocks, down, 0)
-    send_back(dblocks - 1)
-    sent(dblocks - 2)
-    sent(dblocks - 1)
+    last = dblocks - 1
+    lax.fori_loop(0, last, down, 0)
+    slot = (n_ad + last) % SLOTS
+    send_back(last - 1)
+    sent(last - 2)
+    for c in d_copies(last, slot):
+        c.wait()
+    down_rows(last, slot, 0, half, kk)
+    down_rows(last, slot, half, half // 2, kh)
+    remote, local = back_copies(last)
+    for m in remote:
+        m.start()
+    down_rows(last, slot, half + half // 2, half // 2, kh)
+    local.start()
+    sent(last - 1)
+    sent(last)
     for off in (2, 3, 1):
         rows = pl.ds((off - 1) * cap, cap)
         pltpu.make_async_remote_copy(
@@ -397,8 +384,8 @@
             device_id={"data": peer_of(me, off)}, device_id_type=MESH).wait_recv()
 
 
-def mlp(scale, cap, xs, sel, ws, cold, hot):
-    toks, d = xs.shape
+def mlp(scale, cap, n_local, hot_ids, ids, x, ws, cold, hot):
+    toks, d = x.shape
     f = ws[0].shape[1]
     kh, kc = hot[0].shape[0], cold[0].shape[0]
     kk = kh + kc
@@ -406,13 +393,16 @@
     pairs = [m for h, c in zip(hot, cold) for m in (h, c)]
     dma = pltpu.SemaphoreType.DMA
     return pl.pallas_call(
-        functools.partial(mlp_kernel, scale, cap),
-        in_specs=[pl.BlockSpec(memory_space=pl.ANY)] * 17,
-        out_specs=pl.BlockSpec(memory_space=pl.ANY),
-        out_shape=jax.ShapeDtypeStruct((toks, d), BF),
+        functools.partial(mlp_kernel, scale, cap, n_local),
+        in_specs=[pl.BlockSpec(memory_space=pltpu.SMEM), pl.BlockSpec(memory_space=pltpu.VMEM)] + [pl.BlockSpec(memory_space=pl.ANY)] * 16,
+        out_specs=[pl.BlockSpec(memory_space=pl.ANY)] * 2,
+        out_shape=[jax.ShapeDtypeStruct((toks, d), BF), jax.ShapeDtypeStruct((toks, toks), BF)],
         scratch_shapes=[
             pltpu.VMEM((toks, d), BF),
             pltpu.VMEM((toks, 128), BF),
+            pltpu.VMEM((half, 128), BF),
+            pltpu.VMEM((toks, toks), BF),
+            pltpu.VMEM((toks, toks), BF),
             pltpu.VMEM((toks, f), BF),
             pltpu.VMEM((SLOTS, f, FB), BF),
             pltpu.VMEM((SLOTS, 2, kk, FB), BF),
@@ -422,12 +412,12 @@
             pltpu.VMEM((toks, kh), F32),
             pltpu.VMEM((half, kc), F32),
             pltpu.VMEM((2, toks, FB), BF),
-            dma((2,)), dma((3,)), dma((3,)), dma((2,)), dma((3,)), dma((3,)),
+            dma((d // 1024,)), dma, dma((3,)), dma((3,)), dma((3,)), dma((3,)),
             dma((SLOTS, 2)), dma((SLOTS, 4)), dma((SLOTS, 2 * (f // FB // AD_STEPS))), dma((3,)), dma((2, 3)), dma((3,)), dma((2,)),
         ],
         compiler_params=pltpu.CompilerParams(
             collective_id=0, has_side_effects=True, vmem_limit_bytes=63 * 1024 * 1024),
-    )(xs, sel, *ws, *pairs)
+    )(hot_ids, ids.reshape(1, toks), x, *ws, *pairs)
 
 
 def solution(mesh):
@@ -448,10 +438,9 @@
         def flat_b(b):
             return b.reshape(-1, b.shape[2])
 
-        xs, sel, back = route(x, adapter_id, hot_ids, a_gate.shape[0], cap)
         cold = [flat_a(a_gate), flat_b(b_gate), flat_a(a_up), flat_b(b_up), flat_a(a_down), flat_b(b_down)]
         hot = [flat_a(hot_a_gate), flat_b(hot_b_gate), flat_a(hot_a_up), flat_b(hot_b_up), flat_a(hot_a_down), flat_b(hot_b_down)]
-        ys = mlp(scale, cap, xs, sel, (w_gate, w_up, w_down), cold, hot)
+        ys, back = mlp(scale, cap, a_gate.shape[0], hot_ids, adapter_id, x, (w_gate, w_up, w_down), cold, hot)
         return unroute(back, ys)
 
     return jax.shard_map(device_step, mesh=mesh, in_specs=in_specs, out_specs=token_spec, check_vma=False)

time: 324 us -> 318 us (0.981)
  Pallas kernels: 324 us -> 318 us
    pallas_call x2 -> x1, Pallas kernels: 316 us -> 311 us  [mlp(): pl.pallas_call(functools.partial(mlp_kernel, scale, cap, n_local), in_spe...]
where the time goes in v3:
time: 318 us
  Pallas kernels  318 us (100%)
    pallas_call x1, Pallas kernels, mlp(): pl.pallas_call(functools.partial(mlp_kernel, scale, cap, n_local), in_spe...  311 us
    pallas_call x1, Pallas kernels, unroute(): pl.pallas_call(unroute_kernel, grid=(width // chunk,), in_specs=[pl.Block...  6.97 us

profile of v3, /device:TPU:0, one launch (start us, length us, event | category | flops | bytes accessed | tf_op | source)
XLA Modules:
  0.0 318.1 jit_solution(5364991833111324442)
XLA Ops:
  0.0 311.1 %shard_map.172 = (bf16[512,5120]{1,0:T(8,128)(2,1)}, bf16[512,512]{1,0:T(8,128)(2,1)}) custom-call(s32[4]{0:T(128)} %hot_ids.1, s32[1,512]{1,0:T(1,128)} %bitcast.37, bf16[512,5120]{1,0:T(8,128)(2,1)} %x.1, bf16[5120,13824]{1,0:T(8,128)(2,1)} %wg.1, bf16[5120,13824]{1,0:T(8,128)(2,1)} %wu.1, bf16[13824,5120]{1,0:T(8,128)(2,1)} %wd.1, ...), custom_call_target="tpu_custom_call" | custom-call | tf_op jit(solution)/shard_map/pallas_call | solution.py:395
  311.1 7.0 %shard_map.173 = bf16[512,5120]{1,0:T(8,128)(2,1)} custom-call(bf16[512,512]{1,0:T(8,128)(2,1)} %get-tuple-element.7.back_ref, bf16[512,5120]{1,0:T(8,128)(2,1)} %get-tuple-element.8.ys_ref), custom_call_target="tpu_custom_call" | custom-call | tf_op jit(solution)/shard_map/pallas_call | solution.py:71
